TPU v7x, 32 devices: a whole 2x2x4 slice. The times are simulated.
32 devices in a mesh: ep: 2 (over y), tp: 16 (over z, x, core).
Axes of the slice: x: 2, y: 2, z: 4, core: 2. Of those that a mesh axis runs over, the one named last changes fastest.
Arguments:
- activations: bfloat16 [64, 6144], P(None, 'tp'), may hold values from -6 to 6
- norm_gain: float32 [6144], replicated, may hold values from 0.1 to 1.9
- router_weight: bfloat16 [6144, 8], P('tp'), may hold values from -0.078125 to 0.078125
- expert_ids: int32 [64, 2], replicated, may hold values from 0 to 7, all different within a row
- w_gate: bfloat16 [8, 6144, 2048], P('ep', None, 'tp'), may hold values from -0.078125 to 0.078125
- w_up: bfloat16 [8, 6144, 2048], P('ep', None, 'tp'), may hold values from -0.078125 to 0.078125
- w_down: bfloat16 [8, 2048, 6144], P('ep', 'tp'), may hold values from -0.1875 to 0.1875
Outputs:
- moe_out: bfloat16 [64, 6144], P(None, 'tp')
Inputs may be any that keep to these rules, and one draw needn't show every extreme that they name: `expert_ids`: each row names two different experts from 0 to 7, and every expert is named by some token.
All inputs are finite; a program needn't handle non-finite values.
Results may differ from a plain program's by a relative error of at most 0.0025.
Values may be sent and summed in bfloat16 or wider, within the bound.
A program may use at most 64 MiB of HBM per device.

v0:
```python
import jax
import jax.numpy as jnp
from jax import lax
from jax.sharding import PartitionSpec as P

epsilon = 1e-05


def summed_rows(portion, rows, axis):
    count = rows * lax.axis_size(axis)
    return lax.psum_scatter(portion(jnp.int32(0), count), axis, scatter_dimension=0, tiled=True)


def shards(activations, norm_gain, router_weight, expert_ids, w_gate, w_up, w_down):
    shard_width = activations.shape[1]
    gathered = lax.all_gather(activations, "tp", axis=1, tiled=True)
    features = gathered.astype(jnp.float32)
    inv_rms = lax.rsqrt(jnp.mean(features * features, axis=1, keepdims=True) + epsilon)
    normed = (features * inv_rms * norm_gain.astype(jnp.float32)).astype(jnp.bfloat16)
    router_full = lax.all_gather(router_weight, "tp", axis=0, tiled=True)
    logits = jnp.dot(normed, router_full, preferred_element_type=jnp.float32)
    expert_total = router_weight.shape[1]
    chosen = jnp.take_along_axis(logits, expert_ids, axis=1)
    weights = jax.nn.softmax(chosen, axis=1)
    gate_dense = jnp.sum(
        weights[:, :, None] * jax.nn.one_hot(expert_ids, expert_total, dtype=jnp.float32), axis=1
    )
    local_count = w_gate.shape[0]
    local_gates = lax.dynamic_slice_in_dim(
        gate_dense, lax.axis_index("ep") * local_count, local_count, 1
    )
    gate_per_expert = local_gates.T
    gate_act = jnp.einsum("td,edf->etf", normed, w_gate, preferred_element_type=jnp.float32)
    up_act = jnp.einsum("td,edf->etf", normed, w_up, preferred_element_type=jnp.float32)
    hidden = (jax.nn.silu(gate_act) * up_act).astype(jnp.bfloat16)

    def weighted_terms(begin_row, row_count):
        columns = lax.dynamic_slice_in_dim(w_down, begin_row, row_count, 2)
        products = jnp.einsum("efc,etf->ect", columns, hidden, preferred_element_type=jnp.float32)
        return jnp.sum(products * gate_per_expert[:, None, :], axis=0)

    own_rows = summed_rows(weighted_terms, shard_width, "tp")
    summed = lax.psum(own_rows, "ep")
    return summed.T.astype(jnp.bfloat16)


def solution(mesh):
    in_specs = (
        P(None, "tp"),
        P(),
        P("tp", None),
        P(),
        P("ep", None, "tp"),
        P("ep", None, "tp"),
        P("ep", "tp", None),
    )
    out_specs = P(None, "tp")
    return jax.shard_map(shards, mesh=mesh, in_specs=in_specs, out_specs=out_specs, check_vma=False)
```

profile of v0, /device:TPU:0, one launch (start us, length us, event | category | flops | bytes accessed | tf_op | source)
XLA Modules:
  0.0 141.0 jit_solution(3283291192828274340)
XLA Ops:
  6.5 0.0 copy-start
  6.5 0.0 reduce-scatter.2.cloned.1.call-start
  6.5 0.7 bitcast_or_fusion
  7.2 0.1 copy.32
  7.3 0.1 reshape.41
  7.5 23.6 %all_gather.7 = bf16[6144,8]{0,1:T(8,128)(2,1)S(1)} all-gather(bf16[384,8]{0,1:T(8,128)(2,1)} %param.9), channel_id=1, replica_groups=mesh['ep'=2,'tp'=16] {'tp'}, dimensions={0}, use_global_device_ids=true | all-gather | bytes 104448 | tf_op jit(solution)/shard_map/all_gather | solution.py:20
  31.1 19.8 %all_gather.6 = bf16[64,6144]{1,0:T(8,128)(2,1)S(1)} all-gather(bf16[64,384]{1,0:T(8,128)(2,1)} %param.7), channel_id=1, replica_groups=mesh['ep'=2,'tp'=16] {'tp'}, dimensions={1}, use_global_device_ids=true | all-gather | bytes 835584 | tf_op jit(solution)/shard_map/all_gather | solution.py:16
  50.9 0.3 fusion.1
  51.1 0.0 copy-done
  51.1 0.4 fusion.21
  51.5 0.0 copy-start.1
  51.5 1.0 gather_fusion
  52.6 0.1 reshape.44
  52.7 0.1 copy.33
  52.8 0.0 copy-done.1
  52.9 4.0 %convolution_bitcast_fusion.1 = f32[4,64,128]{2,1,0:T(8,128)S(1)} fusion(bf16[4,6144,128]{2,1,0:T(8,128)(2,1)} %param.11, bf16[64,6144]{1,0:T(8,128)(2,1)S(1)} %all_gather.6, f32[6144]{0:T(1024)S(1)} %copy-done, f32[64]{0:T(128)S(1)} %add_rsqrt_fusion), kind=kOutput, calls=%fused_computation.10 | convolution fusion | flops 404226048 | bytes 7233792 | tf_op jit(solution)/shard_map/td,edf->etf/dot_general | solution.py:33
  56.9 8.7 %fusion = f32[64,6144]{1,0:T(8,128)} fusion(f32[4,64]{1,0:T(4,128)S(1)} %dynamic-slice_bitcast_fusion, bf16[4,128,6144]{2,1,0:T(8,128)(2,1)} %param.13, bf16[4,6144,128]{2,1,0:T(8,128)(2,1)} %param.12, f32[4,64,128]{2,1,0:T(8,128)S(1)} %convolution_bitcast_fusion.1, bf16[64,6144]{1,0:T(8,128)(2,1)S(1)} %all_gather.6, f32[6144]{0:T(1024)S(1)} %copy-done, ...), kind=kOutput, calls=%fused_computation.2 | convolution fusion | flops 809828352 | bytes 15099136 | tf_op jit(solution)/shard_map/efc,etf->ect/dot_general | solution.py:39
  65.7 0.0 reduce-scatter.2.cloned.1.call-update
  65.7 58.0 %reduce-scatter.2.cloned.1.call-done = f32[384,64]{0,1:T(8,128)} async-done(((f32[6144,64]{0,1:T(8,128)}), f32[384,64]{0,1:T(8,128)}) %reduce-scatter.2.cloned.1.call-update) | async-done | bytes 98320 | tf_op jit(solution)/shard_map/reduce_scatter | solution.py:11
  123.7 10.4 %psum.7 = bf16[384,64]{0,1:T(8,128)(2,1)} all-reduce(f32[384,64]{0,1:T(8,128)} %reduce-scatter.2.cloned.1.call-done), channel_id=1, replica_groups=mesh['ep'=2,'tp'=16] {'ep'}, use_global_device_ids=true, to_apply=%region_6.7 | all-reduce | flops 24576 | bytes 147456 | tf_op jit(solution)/shard_map/psum | solution.py:43
  (6 shorter events, 0.1 us)
Async XLA Ops:
  6.5 44.6 %copy-start = (f32[6144]{0:T(1024)S(1)}, f32[6144]{0:T(1024)}, u32[]{:S(2)}) copy-start(f32[6144]{0:T(1024)} %param.8) | copy-start | bytes 73732
  6.5 117.2 %reduce-scatter.2.cloned.1.call-start = ((), (), s32[]{:S(2)}) async-start(), calls=%async_computation.1 | async-start | bytes 1671168 | tf_op jit(solution)/shard_map/reduce_scatter | solution.py:11
  51.5 1.2 copy-start.1
Sparse Core Ops, SparseCore 0:
  65.8 57.8 reduce-scatter.1
where the time goes:
time: 141 us
  waiting for transfers between devices  58.1 us (41%)
  blocking collectives  53.8 us (38%)
  between operations  13.5 us (10%)
  matrix products  13.2 us (9%)
  local copies, waits for them, and re-layouts  1.47 us (1%)
    reduce_scatter x1, waiting for transfers between devices, summed_rows(): lax.psum_scatter(portion(jnp.int32(0), count), axis, scatter_dimension=0,...  58 us
    all_gather x1, blocking collectives, shards(): router_full = lax.all_gather(router_weight, 'tp', axis=0, tiled=True)  23.6 us
    all_gather x1, blocking collectives, shards(): gathered = lax.all_gather(activations, 'tp', axis=1, tiled=True)  19.8 us
    psum x1, blocking collectives, shards(): summed = lax.psum(own_rows, 'ep')  10.4 us
    dot_general x1, matrix products, weighted_terms(): jnp.einsum('efc,etf->ect', columns, hidden, preferred_element_type=jnp.fl...  8.72 us
    dot_general x1, matrix products, shards(): jnp.einsum('td,edf->etf', normed, w_gate, preferred_element_type=jnp.floa...  4.05 us
  transfers between devices with their start and end apart: 1, of which 1 were waited for; matrix products, arithmetic and copies ran while one was open for 0% of the time, Pallas kernels for 0%

commit v1 on v0

--- a/solution.py
+++ b/solution.py
@@ -1,9 +1,281 @@
+import functools
+
 import jax
 import jax.numpy as jnp
 from jax import lax
+from jax.experimental import pallas as pl
+from jax.experimental.pallas import tpu as pltpu
 from jax.sharding import PartitionSpec as P
 
 epsilon = 1e-05
+MESH = pl.DeviceIdType.MESH
+
+
+def layer_kernel(
+    lines, local_count, x_hbm, gain_hbm, r_hbm, ids_hbm, wg_hbm, wu_hbm, wd_hbm, o_ref,
+    x_all, r_all, gain, ids, wgu, wd, normed, rwide,
+    pair_out, pair_in, own, ep_out, ep_in, side_out, side_in, line_out, line_in, last_out, last_in,
+    load_sem, gu_sem, down_sem,
+    z_send, z_recv, s_send, s_recv, c_send, c_recv,
+    pair_ss, pair_rs, ep_ss, ep_rs, side_ss, side_rs, line_ss, line_rs, last_ss, last_rs,
+):
+    rows, width = x_all.shape[1], x_all.shape[2]
+    half = rows // 2
+    y = lax.axis_index("ep")
+    t = lax.axis_index("tp")
+    c = t % 2
+    x = (t // 2) % 2
+    z = t // 4
+
+    def index(zz, xx, cc):
+        return (zz * 2 + xx) * 2 + cc
+
+    def at_z(step):
+        return (z + step) % lines
+
+    pair = (y, index(z, x, 1 - c))
+    side = (y, index(z, 1 - x, c))
+    other = (1 - y, t)
+
+    def along(step):
+        return (y, index(at_z(step), x, c))
+
+    loads = [
+        pltpu.make_async_copy(x_hbm, x_all.at[t], load_sem.at[0]),
+        pltpu.make_async_copy(r_hbm, r_all.at[t], load_sem.at[1]),
+        pltpu.make_async_copy(gain_hbm, gain, load_sem.at[2]),
+        pltpu.make_async_copy(ids_hbm, ids, load_sem.at[3]),
+    ]
+    for load in loads:
+        load.start()
+    inner = wg_hbm.shape[2]
+    gu_loads = []
+    for e in range(local_count):
+        gu_loads.append(pltpu.make_async_copy(wg_hbm.at[e], wgu.at[e, :, pl.ds(0, inner)], gu_sem.at[e, 0]))
+        gu_loads.append(pltpu.make_async_copy(wu_hbm.at[e], wgu.at[e, :, pl.ds(inner, inner)], gu_sem.at[e, 1]))
+    for load in gu_loads:
+        load.start()
+    down_load = pltpu.make_async_copy(wd_hbm, wd, down_sem.at[0])
+    down_load.start()
+
+    barrier = pltpu.get_barrier_semaphore()
+    peers = [pair, side, other] + [along(step) for step in range(1, lines)]
+    for peer in peers:
+        pl.semaphore_signal(barrier, inc=1, device_id=peer, device_id_type=MESH)
+    pl.semaphore_wait(barrier, len(peers))
+
+    def remote(src, dst, ss, rs, peer):
+        return pltpu.make_async_remote_copy(
+            src_ref=src, dst_ref=dst, send_sem=ss, recv_sem=rs, device_id=peer, device_id_type=MESH
+        )
+
+    sent = []
+
+    def gather(buf, kind):
+        def block(i):
+            return buf.at[i]
+
+        zs, ss, cs = [], [], []
+        for step in range(1, lines):
+            zs.append(remote(block(t), block(t), z_send.at[kind, step], z_recv.at[kind, step], along(step)))
+        for k in range(lines):
+            held = block(index(at_z(lines - k), x, c))
+            ss.append(remote(held, held, s_send.at[kind, k], s_recv.at[kind, k], side))
+            mine = [held, block(index(at_z(lines - k), 1 - x, c))]
+            cs.append([remote(h, h, c_send.at[kind, k, n], c_recv.at[kind, k, n], pair) for n, h in enumerate(mine)])
+        return zs, ss, cs
+
+    gx, gr = gather(x_all, 0), gather(r_all, 1)
+    order = [0] + sorted(range(1, lines), key=lambda k: (min(k, lines - k), k))
+    for (zs, ss, cs), load in ((gx, loads[0]), (gr, loads[1])):
+        load.wait()
+        for step in order[:0:-1]:
+            zs[step - 1].start()
+        ss[0].start()
+        cs[0][0].start()
+    for zs, ss, cs in (gx, gr):
+        ss[0].wait_recv()
+        cs[0][1].start()
+        for k in order[1:]:
+            zs[k - 1].wait_recv()
+            ss[k].start()
+            cs[k][0].start()
+        for k in order[1:]:
+            ss[k].wait_recv()
+            cs[k][1].start()
+    for group in gx[2]:
+        for copy in group:
+            copy.wait_recv()
+
+    loads[2].wait()
+    blocks = x_all.shape[0]
+    total = jnp.zeros((rows, width), jnp.float32)
+    for b in range(blocks):
+        f = x_all[b].astype(jnp.float32)
+        total = total + f * f
+    inv_rms = lax.rsqrt(jnp.sum(total, axis=1, keepdims=True) / (blocks * width) + epsilon)
+    for b in range(blocks):
+        cols = pl.ds(b * width, width)
+        normed[:, cols] = (x_all[b].astype(jnp.float32) * inv_rms * gain[:, cols]).astype(jnp.bfloat16)
+
+    hidden = []
+    for e in range(local_count):
+        gu_loads[2 * e].wait()
+        gu_loads[2 * e + 1].wait()
+        acts = jnp.dot(normed[...], wgu[e], preferred_element_type=jnp.float32)
+        gate_act, up_act = acts[:, :inner], acts[:, inner:]
+        hidden.append((gate_act / (1.0 + jnp.exp(-gate_act)) * up_act).astype(jnp.bfloat16))
+
+    for group in gr[2]:
+        for copy in group:
+            copy.wait_recv()
+    for b in range(blocks):
+        rwide[:, pl.ds(b * width, width)] = r_all[b]
+    logits = lax.dot_general(
+        normed[...], rwide[...], (((1,), (1,)), ((), ())), preferred_element_type=jnp.float32
+    )
+    loads[3].wait()
+    eye = lax.broadcasted_iota(jnp.int32, (rows, rows), 0) == lax.broadcasted_iota(jnp.int32, (rows, rows), 1)
+    lane = lax.broadcasted_iota(jnp.int32, logits.shape, 1).astype(jnp.float32)
+    picks, chosen = [], []
+    for k in range(2):
+        row = ids[pl.ds(k, 1), :].astype(jnp.float32)
+        pick = jnp.sum(jnp.where(eye, row, 0.0), axis=1, keepdims=True)
+        picks.append(pick)
+        chosen.append(jnp.sum(jnp.where(lane == pick, logits, 0.0), axis=1, keepdims=True))
+    top = jnp.maximum(chosen[0], chosen[1])
+    powers = [jnp.exp(v - top) for v in chosen]
+    weights = [v / (powers[0] + powers[1]) for v in powers]
+    gates = []
+    for e in range(local_count):
+        number = (y * local_count + e).astype(jnp.float32)
+        gates.append(
+            jnp.where(picks[0] == number, weights[0], 0.0) + jnp.where(picks[1] == number, weights[1], 0.0)
+        )
+    down_load.wait()
+
+    def partial(owner):
+        cols = pl.ds(pl.multiple_of(owner * width, width), width)
+        out = None
+        for e in range(local_count):
+            term = gates[e] * jnp.dot(hidden[e], wd[e, :, cols], preferred_element_type=jnp.float32)
+            out = term if out is None else out + term
+        return out
+
+    offsets = [k for k in order[::-1]]
+    count = 2 * lines
+    pairs = [remote(pair_out.at[m], pair_in.at[m], pair_ss.at[m], pair_rs.at[m], pair) for m in range(count)]
+    eps = [remote(ep_out.at[m], ep_in.at[m], ep_ss.at[m], ep_rs.at[m], other) for m in range(count)]
+    sides = [remote(side_out.at[j], side_in.at[j], side_ss.at[j], side_rs.at[j], side) for j in range(lines)]
+    line = [
+        remote(line_out.at[j], line_in.at[j], line_ss.at[j], line_rs.at[j], along(offsets[j])) if offsets[j] else None
+        for j in range(lines)
+    ]
+    mine = pl.ds(pl.multiple_of(y * half, half), half)
+    theirs = pl.ds(pl.multiple_of((1 - y) * half, half), half)
+
+    def make(m):
+        zz, xx = at_z(offsets[m // 2]), (1 - x if m % 2 == 0 else x)
+        pair_out[m] = partial(index(zz, xx, 1 - c))
+        pairs[m].start()
+        own[m] = partial(index(zz, xx, c))
+
+    def over_ep(m):
+        pairs[m].wait_recv()
+        ep_out[m] = (own[m, theirs, :] + pair_in[m, theirs, :]).astype(jnp.bfloat16)
+        eps[m].start()
+
+    def half_sum(m):
+        return own[m, mine, :] + pair_in[m, mine, :] + ep_in[m].astype(jnp.float32)
+
+    def over_side(j):
+        eps[2 * j].wait_recv()
+        side_out[j] = half_sum(2 * j)
+        sides[j].start()
+
+    kept = []
+
+    def over_line(j):
+        eps[2 * j + 1].wait_recv()
+        sides[j].wait_recv()
+        value = half_sum(2 * j + 1) + side_in[j]
+        if offsets[j]:
+            line_out[j] = value
+            line[j].start()
+        else:
+            kept.append(value)
+
+    for s in range(count + 11):
+        if s < count:
+            make(s)
+        if 0 <= s - 1 < count:
+            over_ep(s - 1)
+        if s >= 5 and (s - 5) % 2 == 0 and (s - 5) // 2 < lines:
+            over_side((s - 5) // 2)
+        if s >= 9 and (s - 9) % 2 == 0 and (s - 9) // 2 < lines:
+            over_line((s - 9) // 2)
+    result = kept[0]
+    for j in range(lines):
+        if offsets[j]:
+            line[j].wait_recv()
+            result = result + line_in[j]
+    last_out[...] = result.astype(jnp.bfloat16)
+    last = remote(last_out, last_in, last_ss.at[0], last_rs.at[0], other)
+    last.start()
+    o_ref[mine, :] = result.astype(jnp.bfloat16)
+    for zs, ss, cs in (gx, gr):
+        for copy in zs + ss + [copy for group in cs for copy in group]:
+            copy.wait_send()
+    for copy in pairs + eps + sides + [copy for copy in line if copy is not None]:
+        copy.wait_send()
+    last.wait()
+    o_ref[theirs, :] = last_in[...]
+
+
+def fused_shards(lines, activations, norm_gain, router_weight, expert_ids, w_gate, w_up, w_down):
+    rows, width = activations.shape
+    blocks = 4 * lines
+    count = 2 * lines
+    local_count, features, inner = w_gate.shape
+    experts = router_weight.shape[1]
+    half = rows // 2
+    f32, bf16 = jnp.float32, jnp.bfloat16
+    dma = pltpu.SemaphoreType.DMA
+    return pl.pallas_call(
+        functools.partial(layer_kernel, lines, local_count),
+        out_shape=jax.ShapeDtypeStruct((rows, width), bf16),
+        in_specs=[pl.BlockSpec(memory_space=pltpu.HBM)] * 7,
+        out_specs=pl.BlockSpec(memory_space=pltpu.VMEM),
+        scratch_shapes=[
+            pltpu.VMEM((blocks, rows, width), bf16),
+            pltpu.VMEM((blocks, experts, width), bf16),
+            pltpu.VMEM((1, features), f32),
+            pltpu.VMEM(expert_ids.shape[::-1], jnp.int32),
+            pltpu.VMEM((local_count, features, 2 * inner), bf16),
+            pltpu.VMEM(w_down.shape, bf16),
+            pltpu.VMEM((rows, features), bf16),
+            pltpu.VMEM((experts, features), bf16),
+            pltpu.VMEM((count, rows, width), f32),
+            pltpu.VMEM((count, rows, width), f32),
+            pltpu.VMEM((count, rows, width), f32),
+            pltpu.VMEM((count, half, width), bf16),
+            pltpu.VMEM((count, half, width), bf16),
+            pltpu.VMEM((lines, half, width), f32),
+            pltpu.VMEM((lines, half, width), f32),
+            pltpu.VMEM((lines, half, width), f32),
+            pltpu.VMEM((lines, half, width), f32),
+            pltpu.VMEM((half, width), bf16),
+            pltpu.VMEM((half, width), bf16),
+            dma((4,)), dma((local_count, 2)), dma((1,)),
+            dma((2, lines)), dma((2, lines)), dma((2, lines)), dma((2, lines)),
+            dma((2, lines, 2)), dma((2, lines, 2)),
+            dma((count,)), dma((count,)), dma((count,)), dma((count,)),
+            dma((lines,)), dma((lines,)), dma((lines,)), dma((lines,)), dma((1,)), dma((1,)),
+        ],
+        compiler_params=pltpu.CompilerParams(
+            collective_id=0, has_side_effects=True, vmem_limit_bytes=60 * 1024 * 1024
+        ),
+    )(activations, norm_gain.astype(f32).reshape(1, -1), router_weight.T, expert_ids.T, w_gate, w_up, w_down)
 
 
 def summed_rows(portion, rows, axis):
@@ -45,6 +317,7 @@
 
 
 def solution(mesh):
+    tp = mesh.shape["tp"]
     in_specs = (
         P(None, "tp"),
         P(),
@@ -55,4 +328,11 @@
         P("ep", "tp", None),
     )
     out_specs = P(None, "tp")
-    return jax.shard_map(shards, mesh=mesh, in_specs=in_specs, out_specs=out_specs, check_vma=False)
+
+    def plan(activations, *rest):
+        fits = tp % 4 == 0 and mesh.shape["ep"] == 2 and activations.shape[1] % 128 == 0
+        fits = fits and activations.shape[0] % 32 == 0 and rest[3].shape[2] % 128 == 0
+        part = functools.partial(fused_shards, tp // 4) if fits else shards
+        return part(activations, *rest)
+
+    return jax.shard_map(plan, mesh=mesh, in_specs=in_specs, out_specs=out_specs, check_vma=False)

time: 141 us -> 43.5 us (0.31)
  waiting for transfers between devices: 58.1 us -> 0 us
  blocking collectives: 53.8 us -> 0 us
  Pallas kernels: 0 us -> 42 us
  between operations: 13.5 us -> 0.01 us
  matrix products: 13.2 us -> 0 us
    reduce_scatter x1 -> x0, waiting for transfers between devices: 58 us -> none  [summed_rows(): lax.psum_scatter(portion(jnp.int32(0), count), axis, scatter_dimension=0,...]
    all_gather x2 -> x0, blocking collectives: 43.4 us -> none  [the longest x1 23.6 us: shards(): router_full = lax.all_gather(router_weight, 'tp', axis=0, tiled=True)]
    pallas_call x0 -> x1, Pallas kernels: none -> 42 us  [fused_shards(): pl.pallas_call(functools.partial(layer_kernel, lines, local_count), out_s...]
    dot_general x3 -> x0, matrix products: 13.2 us -> none  [the longest x1 8.72 us: weighted_terms(): jnp.einsum('efc,etf->ect', columns, hidden, preferred_element_type=jnp.fl...]
    psum x1 -> x0, blocking collectives: 10.4 us -> none  [shards(): summed = lax.psum(own_rows, 'ep')]
    gather x5 -> x0, local copies, waits for them, and re-layouts: 1.46 us -> none  [shards(): chosen = jnp.take_along_axis(logits, expert_ids, axis=1)]
    unnamed x4 -> x1, local copies, waits for them, and re-layouts: 0.01 us -> 1.42 us
  transfers between devices with their start and end apart: 1 -> 0, of which waited for: 1 -> 0; matrix products, arithmetic and copies ran while one was open for 0% -> 0% of each run, Pallas kernels for 0% -> 0%
where the time goes in v1:
time: 43.5 us; the launch traced here: 43.4 us
  Pallas kernels  42 us (97%)
  local copies, waits for them, and re-layouts  1.42 us (3%)
    pallas_call x1, Pallas kernels, fused_shards(): pl.pallas_call(functools.partial(layer_kernel, lines, local_count), out_s...  42 us
    unnamed x1, local copies, waits for them, and re-layouts  1.42 us

profile of v1, /device:TPU:0, one launch (start us, length us, event | category | flops | bytes accessed | tf_op | source)
XLA Modules:
  0.0 43.4 jit_solution(15297733830086068182)
XLA Ops:
  0.0 42.0 %shard_map.73 = bf16[64,384]{1,0:T(8,128)(2,1)} custom-call(bf16[64,384]{1,0:T(8,128)(2,1)} %x_hbm.1, f32[1,6144]{1,0:T(1,128)} %bitcast.3, bf16[8,384]{1,0:T(8,128)(2,1)} %bitcast.4, s32[2,64]{1,0:T(2,128)} %bitcast.5, bf16[4,6144,128]{2,1,0:T(8,128)(2,1)} %wg_hbm.1, bf16[4,6144,128]{2,1,0:T(8,128)(2,1)} %wu_hbm.1, bf16[4,128,6144]{2,1,0:T(8,128)(2,1)} %wd_hbm.1), custom_call_target="tpu_custom_call" | custom-call | tf_op jit(solution)/shard_map/pallas_call | solution.py:244
  42.0 1.4 %copy.9 = bf16[64,384]{1,0:T(8,128)(2,1)} copy(bf16[64,384]{1,0:T(8,128)(2,1)} %shard_map.73) | data formatting | bytes 98304
